TPU v7x, 32 devices: a whole 2x2x4 slice. The times are simulated.
32 devices in a mesh: row: 8 (over z, core), col: 4 (over y, x).
Axes of the slice: x: 2, y: 2, z: 4, core: 2. Of those that a mesh axis runs over, the one named last changes fastest.
Arguments:
- signal: float32 [128, 128, 256], P(None, 'row', 'col'), may hold values from -6 to 6
- symbol_x: float32 [128], replicated, may hold values from 0.3 to 3
- symbol_y: float32 [128], replicated, may hold values from 0.3 to 3
- symbol_z: float32 [256], replicated, may hold values from 0.3 to 3
Outputs:
- modes: float32 [128, 128, 256], P('row', 'col')
All inputs are finite; a program needn't handle non-finite values.
Results may differ from a plain program's by a relative error of at most 0.0003.
Values sent between devices are 32-bit elements.
A program may use at most 64 MiB of HBM per device.

v0:
```python
import jax
import jax.numpy as jnp
from jax import lax
from jax.sharding import PartitionSpec as P


def mode_table(count):
    rank = jnp.arange(count)
    angle = 2.0 * jnp.pi / count * (rank[:, None] * rank[None, :] % count).astype(jnp.float32)
    return (jnp.cos(angle) + jnp.sin(angle)) * count ** (-0.5)


def transform_dim(values, dim):
    moved = jnp.tensordot(
        values, mode_table(values.shape[dim]), axes=([dim], [0]), precision=lax.Precision.HIGHEST
    )
    return jnp.moveaxis(moved, -1, dim)


def on_device(signal, symbol_x, symbol_y, symbol_z):

    def first_leg(part_values):
        part_values = transform_dim(part_values, 0)
        part_values = lax.all_to_all(part_values, "row", split_axis=0, concat_axis=1, tiled=True)
        part_values = transform_dim(part_values, 1)
        return part_values

    block_values = first_leg(signal)
    block_values = lax.all_to_all(block_values, "col", split_axis=1, concat_axis=2, tiled=True)
    block_values = transform_dim(block_values, 2)
    share_x = block_values.shape[0]
    part_x = lax.dynamic_slice_in_dim(symbol_x, lax.axis_index("row") * share_x, share_x)
    share_y = block_values.shape[1]
    part_y = lax.dynamic_slice_in_dim(symbol_y, lax.axis_index("col") * share_y, share_y)
    symbol = part_x[:, None, None] + part_y[None, :, None] + symbol_z[None, None, :]
    block_values = block_values * ((1.0 - 0.2 * symbol) / (1.0 + 0.2 * symbol))
    return block_values


def solution(mesh):
    placed = (P(None, "row", "col"), P(), P(), P())
    return jax.shard_map(
        on_device, mesh=mesh, in_specs=placed, out_specs=P("row", "col", None), check_vma=False
    )
```

profile of v0, /device:TPU:0, one launch (start us, length us, event | category | flops | bytes accessed | tf_op | source)
XLA Modules:
  0.0 49.0 jit_solution(2675580543085098439)
XLA Ops:
  0.0 1.0 %copy-done = f32[128,16,64]{0,2,1:T(8,128)S(1)} copy-done((f32[128,16,64]{0,2,1:T(8,128)S(1)}, f32[128,16,64]{0,2,1:T(8,128)}, u32[]{:S(2)}) %copy-start) | copy-done | bytes 524312
  1.0 0.8 %fusion.26 = f32[128,1024]{0,1:S(1)} fusion(f32[128,1024]{0,1:T(8,128)S(1)} %bitcast.22), kind=kOutput, calls=%fused_computation.32 | convolution fusion | flops 201588736 | bytes 1048576
  1.9 0.5 %copy.12 = f32[128,16,64]{2,1,0:T(8,128)S(1)} copy(f32[128,16,64]{0,2,1:T(8,128)S(1)} %bitcast.27) | data formatting | bytes 1048576 | tf_op jit(solution)/shard_map/dot_general | solution.py:14
  2.4 0.7 %reshape.37 = f32[8,1,16384]{2,1,0:T(1,128)S(1)} reshape(f32[128,16,64]{2,1,0:T(8,128)S(1)} %copy.12) | data formatting | bytes 1048576
  3.1 21.5 %all_to_all.36 = f32[8,1,16384]{2,1,0:T(1,128)S(1)} all-to-all(f32[8,1,16384]{2,1,0:T(1,128)S(1)} %reshape.37), channel_id=1, replica_groups=mesh['row'=8,'col'=4] {'row'}, dimensions={0} | all-to-all | bytes 1048576 | tf_op jit(solution)/shard_map/all_to_all | solution.py:24
  24.5 0.5 %broadcast.76 = f32[]{:T(128)} broadcast(f32[]{:T(128)} %constant.105), dimensions={} | broadcast | bytes 8 | tf_op jit(solution)/shard_map/all_to_all | solution.py:24
  25.0 1.8 %reduce = f32[8,16384]{1,0:T(8,128)S(1)} reduce(f32[8,1,16384]{2,1,0:T(1,128)S(1)} %all_to_all.36, f32[]{:T(128)} %broadcast.76), dimensions={1}, to_apply=%all_to_all.26.reduce_sub_computation | reduce | bytes 1048580 | tf_op jit(solution)/shard_map/all_to_all | solution.py:24
  26.8 0.4 reshape.38
  27.3 0.1 copy.13
  27.4 1.9 %convolution_bitcast_fusion = f32[16,128,64]{1,2,0:T(8,128)S(1)} fusion(f32[16,128,64]{2,1,0:T(8,128)S(1)} %bitcast.25), kind=kOutput, calls=%fused_computation | convolution fusion | flops 201588736 | bytes 1048576 | tf_op jit(solution)/shard_map/dot_general | solution.py:14
  29.3 0.5 %copy.15 = f32[16,128,64]{2,0,1:T(8,128)S(1)} copy(f32[16,128,64]{1,2,0:T(8,128)S(1)} %convolution_bitcast_fusion) | data formatting | bytes 1048576 | tf_op jit(solution)/shard_map/transpose | solution.py:17
  29.8 1.4 %reshape.39 = f32[4,1,32768]{2,1,0:T(1,128)} reshape(f32[128,16,64]{2,1,0:T(8,128)S(1)} %bitcast.23) | data formatting | bytes 1048576
  31.2 3.7 %all-to-all-start.1 = ((f32[4,1,32768]{2,1,0:T(1,128)}), f32[4,1,32768]{2,1,0:T(1,128)S(1)}, u32[]{:S(2)}, u32[]{:S(2)}) async-start(f32[4,1,32768]{2,1,0:T(1,128)} %reshape.39), calls=%async_computation.1 | async-start | bytes 1048576 | tf_op jit(solution)/shard_map/all_to_all | solution.py:29
  34.9 0.7 %copy-done.2 = f32[128]{0:T(128)S(1)} copy-done((f32[128]{0:T(128)S(1)}, f32[128]{0:T(128)}, u32[]{:S(2)}) %copy-start.2) | copy-done | bytes 536
  35.6 0.1 dynamic_slice.7
  35.7 0.7 %copy-done.3 = f32[128]{0:T(128)S(1)} copy-done((f32[128]{0:T(128)S(1)}, f32[128]{0:T(128)}, u32[]{:S(2)}) %copy-start.3) | copy-done | bytes 536
  36.3 0.1 dynamic_slice.6
  36.4 0.1 broadcast_add_fusion
  36.5 6.1 %all-to-all-done.1 = f32[4,1,32768]{2,1,0:T(1,128)S(1)} async-done(((f32[4,1,32768]{2,1,0:T(1,128)}), f32[4,1,32768]{2,1,0:T(1,128)S(1)}, u32[]{:S(2)}, u32[]{:S(2)}) %all-to-all-start.1) | async-done | bytes 524320 | tf_op jit(solution)/shard_map/all_to_all | solution.py:29
  42.6 2.1 %reduce.1 = f32[4,32768]{1,0:T(4,128)S(1)} reduce(f32[4,1,32768]{2,1,0:T(1,128)S(1)} %all-to-all-done.1, f32[]{:T(128)} %broadcast.76), dimensions={1}, to_apply=%all_to_all.30.reduce_sub_computation | reduce | bytes 1048580 | tf_op jit(solution)/shard_map/all_to_all | solution.py:29
  44.7 0.5 %reshape.40 = f32[128,16,64]{2,1,0:T(8,128)S(1)} reshape(f32[4,32768]{1,0:T(4,128)S(1)} %reduce.1) | data formatting | bytes 1048576
  45.2 0.7 %copy.17 = f32[16,32,4,64]{3,2,1,0:T(4,128)S(1)} copy(f32[16,32,4,64]{3,0,1,2:T(8,128)S(1)} %bitcast.26) | data formatting | bytes 1048576 | tf_op jit(solution)/shard_map/all_to_all | solution.py:29
  45.9 0.6 %all_to_all.33 = f32[16,32,256]{2,1,0:T(8,128)S(1)} reshape(f32[16,32,4,64]{3,2,1,0:T(4,128)S(1)} %copy.17) | data formatting | bytes 1048576 | tf_op jit(solution)/shard_map/all_to_all | solution.py:29
  46.6 2.4 %convolution_multiply_fusion = f32[16,32,256]{2,1,0:T(8,128)} fusion(f32[16,32,256]{2,1,0:T(8,128)S(1)} %all_to_all.33, f32[256]{0:T(256)S(1)} %copy-done.1, f32[16,32]{1,0:T(8,128)S(1)} %broadcast_add_fusion), kind=kOutput, calls=%fused_computation.1 | convolution fusion | flops 404488192 | bytes 1051648 | tf_op jit(solution)/shard_map/dot_general | solution.py:14
  (5 shorter events, 0.1 us)
Async XLA Ops:
  0.0 1.0 %copy-start = (f32[128,16,64]{0,2,1:T(8,128)S(1)}, f32[128,16,64]{0,2,1:T(8,128)}, u32[]{:S(2)}) copy-start(f32[128,16,64]{0,2,1:T(8,128)} %param.4) | copy-start | bytes 1572868
  31.2 11.4 %all-to-all-start.1 = ((f32[4,1,32768]{2,1,0:T(1,128)}), f32[4,1,32768]{2,1,0:T(1,128)S(1)}, u32[]{:S(2)}, u32[]{:S(2)}) async-start(f32[4,1,32768]{2,1,0:T(1,128)} %reshape.39), calls=%async_computation.1 | async-start | bytes 1048576 | tf_op jit(solution)/shard_map/all_to_all | solution.py:29
  34.9 0.7 %copy-start.2 = (f32[128]{0:T(128)S(1)}, f32[128]{0:T(128)}, u32[]{:S(2)}) copy-start(f32[128]{0:T(128)} %param.6) | copy-start | bytes 1540
  35.7 0.7 %copy-start.3 = (f32[128]{0:T(128)S(1)}, f32[128]{0:T(128)}, u32[]{:S(2)}) copy-start(f32[128]{0:T(128)} %param.5) | copy-start | bytes 1540
  45.9 0.7 %copy-start.1 = (f32[256]{0:T(256)S(1)}, f32[256]{0:T(256)}, u32[]{:S(2)}) copy-start(f32[256]{0:T(256)} %param.7) | copy-start | bytes 3076
where the time goes:
time: 49.3 us; the launch traced here: 49 us
  blocking collectives  21.5 us (44%)
  local copies, waits for them, and re-layouts  8.49 us (17%)
  waiting for transfers between devices  6.12 us (12%)
  matrix products  5.17 us (10%)
  other arithmetic  3.92 us (8%)
  starting transfers between devices  3.72 us (8%)
    all_to_all x1, blocking collectives, first_leg(): lax.all_to_all(part_values, 'row', split_axis=0, concat_axis=1, tiled=True)  21.5 us
    all_to_all x1, waiting for transfers between devices, on_device(): lax.all_to_all(block_values, 'col', split_axis=1, concat_axis=2, tiled=True)  6.12 us
    unnamed x12, local copies, waits for them, and re-layouts  5.44 us
    dot_general x2, matrix products, transform_dim(): jnp.tensordot(values, mode_table(values.shape[dim]), axes=([dim], [0]), p...  4.32 us
    all_to_all x1, starting transfers between devices, on_device(): lax.all_to_all(block_values, 'col', split_axis=1, concat_axis=2, tiled=True)  3.72 us
    all_to_all x1, other arithmetic, on_device(): lax.all_to_all(block_values, 'col', split_axis=1, concat_axis=2, tiled=True)  2.05 us
    all_to_all x1, other arithmetic, first_leg(): lax.all_to_all(part_values, 'row', split_axis=0, concat_axis=1, tiled=True)  1.8 us
    all_to_all x2, local copies, waits for them, and re-layouts, on_device(): lax.all_to_all(block_values, 'col', split_axis=1, concat_axis=2, tiled=True)  1.29 us
  transfers between devices with their start and end apart: 1, of which 1 were waited for; matrix products, arithmetic and copies ran while one was open for 0% of the time, Pallas kernels for 0%

commit v1 on v0

--- a/solution.py
+++ b/solution.py
@@ -21,7 +21,12 @@
 
     def first_leg(part_values):
         part_values = transform_dim(part_values, 0)
-        part_values = lax.all_to_all(part_values, "row", split_axis=0, concat_axis=1, tiled=True)
+        part_values = jnp.concatenate(
+            lax.all_to_all(
+                jnp.stack(jnp.split(part_values, lax.axis_size("row"), axis=0)), "row", 0, 0
+            ),
+            axis=1,
+        )
         part_values = transform_dim(part_values, 1)
         return part_values
 

time: 49.3 us -> 57.7 us (1.17)
  local copies, waits for them, and re-layouts: 8.49 us -> 16.4 us
    another operation x0 -> x10, local copies, waits for them, and re-layouts: none -> 7.49 us  [first_leg(): jnp.stack(jnp.split(part_values, lax.axis_size('row'), axis=0))]
    unnamed x12 -> x21, local copies, waits for them, and re-layouts: 5.44 us -> 6.33 us
where the time goes in v1:
time: 57.7 us; the launch traced here: 57.3 us
  blocking collectives  21.5 us (37%)
  local copies, waits for them, and re-layouts  16.4 us (28%)
  waiting for transfers between devices  6.19 us (11%)
  matrix products  5.17 us (9%)
  other arithmetic  4.07 us (7%)
  starting transfers between devices  3.72 us (6%)
    all_to_all x1, blocking collectives, first_leg(): lax.all_to_all(jnp.stack(jnp.split(part_values, lax.axis_size('row'), axi...  21.5 us
    another operation x10, local copies, waits for them, and re-layouts, first_leg(): jnp.stack(jnp.split(part_values, lax.axis_size('row'), axis=0))  7.49 us
    unnamed x21, local copies, waits for them, and re-layouts  6.33 us
    all_to_all x1, waiting for transfers between devices, on_device(): lax.all_to_all(block_values, 'col', split_axis=1, concat_axis=2, tiled=True)  6.19 us
    dot_general x2, matrix products, transform_dim(): jnp.tensordot(values, mode_table(values.shape[dim]), axes=([dim], [0]), p...  4.33 us
    all_to_all x1, starting transfers between devices, on_device(): lax.all_to_all(block_values, 'col', split_axis=1, concat_axis=2, tiled=True)  3.72 us
    all_to_all x1, other arithmetic, on_device(): lax.all_to_all(block_values, 'col', split_axis=1, concat_axis=2, tiled=True)  2.13 us
    all_to_all x1, other arithmetic, first_leg(): lax.all_to_all(jnp.stack(jnp.split(part_values, lax.axis_size('row'), axi...  1.87 us
  transfers between devices with their start and end apart: 1, of which 1 were waited for; matrix products, arithmetic and copies ran while one was open for 0% of the time, Pallas kernels for 0%

profile of v1, /device:TPU:0, one launch (start us, length us, event | category | flops | bytes accessed | tf_op | source)
XLA Modules:
  0.0 57.3 jit_solution(10865362876156333967)
XLA Ops:
  0.0 1.0 %copy-done = f32[128,16,64]{0,2,1:T(8,128)S(1)} copy-done((f32[128,16,64]{0,2,1:T(8,128)S(1)}, f32[128,16,64]{0,2,1:T(8,128)}, u32[]{:S(2)}) %copy-start) | copy-done | bytes 524312
  1.0 0.8 %fusion.26 = f32[128,1024]{0,1:S(1)} fusion(f32[128,1024]{0,1:T(8,128)S(1)} %bitcast.36), kind=kOutput, calls=%fused_computation.40 | convolution fusion | flops 201588736 | bytes 1048576
  1.9 2.1 %slice_bitcast_fusion = (f32[1,16,16,64]{1,3,2,0:T(8,128)}, f32[1,16,16,64]{1,3,2,0:T(8,128)}, f32[1,16,16,64]{1,3,2,0:T(8,128)}, f32[1,16,16,64]{1,3,2,0:T(8,12...) fusion(f32[128,16,64]{0,2,1:T(8,128)S(1)} %bitcast.37), kind=kLoop, calls=%fused_computation.2 | loop fusion | bytes 1048576 | tf_op jit(solution)/shard_map/stack | solution.py:26
  4.0 1.2 %copy.29 = f32[1,16,16,64]{3,2,1,0:T(8,128)S(1)} copy(f32[1,16,16,64]{1,3,2,0:T(8,128)} %get-tuple-element.5) | data formatting | bytes 131072 | tf_op jit(solution)/shard_map/stack | solution.py:26
  5.3 1.2 %copy.28 = f32[1,16,16,64]{3,2,1,0:T(8,128)S(1)} copy(f32[1,16,16,64]{1,3,2,0:T(8,128)} %get-tuple-element.6) | data formatting | bytes 131072 | tf_op jit(solution)/shard_map/stack | solution.py:26
  6.5 1.2 %copy.27 = f32[1,16,16,64]{3,2,1,0:T(8,128)S(1)} copy(f32[1,16,16,64]{1,3,2,0:T(8,128)} %get-tuple-element.7) | data formatting | bytes 131072 | tf_op jit(solution)/shard_map/stack | solution.py:26
  7.8 0.8 %copy.26 = f32[1,16,16,64]{3,2,1,0:T(8,128)} copy(f32[1,16,16,64]{1,3,2,0:T(8,128)S(1)} %get-tuple-element.8) | data formatting | bytes 131072 | tf_op jit(solution)/shard_map/stack | solution.py:26
  9.5 0.9 %copy-done.1 = f32[1,16,16,64]{3,2,1,0:T(8,128)S(1)} copy-done((f32[1,16,16,64]{3,2,1,0:T(8,128)S(1)}, f32[1,16,16,64]{3,2,1,0:T(8,128)}, u32[]{:S(2)}) %copy-start.1) | copy-done | bytes 65560
  10.4 0.7 %reshape.45 = f32[8,1,16384]{2,1,0:T(1,128)S(1)} reshape(f32[8,16,16,64]{3,2,1,0:T(8,128)S(1)} %constant_dynamic-update-slice_fusion) | data formatting | bytes 1048576
  11.1 21.5 %all_to_all.23 = f32[8,1,16384]{2,1,0:T(1,128)S(1)} all-to-all(f32[8,1,16384]{2,1,0:T(1,128)S(1)} %reshape.45), channel_id=1, replica_groups=mesh['row'=8,'col'=4] {'row'}, dimensions={0} | all-to-all | bytes 1048576 | tf_op jit(solution)/shard_map/all_to_all | solution.py:25
  32.6 0.6 %broadcast.76 = f32[]{:T(128)} broadcast(f32[]{:T(128)} %constant.128), dimensions={} | broadcast | bytes 8 | tf_op jit(solution)/shard_map/all_to_all | solution.py:25
  33.2 1.9 %reduce = f32[8,16384]{1,0:T(8,128)S(1)} reduce(f32[8,1,16384]{2,1,0:T(1,128)S(1)} %all_to_all.23, f32[]{:T(128)} %broadcast.76), dimensions={1}, to_apply=%all_to_all.16.reduce_sub_computation | reduce | bytes 1048580 | tf_op jit(solution)/shard_map/all_to_all | solution.py:25
  35.6 1.9 %convolution_bitcast_fusion = f32[16,128,64]{1,2,0:T(8,128)S(1)} fusion(f32[16,128,64]{2,1,0:T(8,128)S(1)} %bitcast.40), kind=kOutput, calls=%fused_computation | convolution fusion | flops 201588736 | bytes 1048576 | tf_op jit(solution)/shard_map/dot_general | solution.py:14
  37.5 0.5 copy.32
  38.0 1.4 %reshape.47 = f32[4,1,32768]{2,1,0:T(1,128)} reshape(f32[128,16,64]{2,1,0:T(8,128)S(1)} %bitcast.38) | data formatting | bytes 1048576
  39.4 3.7 %all-to-all-start.1 = ((f32[4,1,32768]{2,1,0:T(1,128)}), f32[4,1,32768]{2,1,0:T(1,128)S(1)}, u32[]{:S(2)}, u32[]{:S(2)}) async-start(f32[4,1,32768]{2,1,0:T(1,128)} %reshape.47), calls=%async_computation.1 | async-start | bytes 1048576 | tf_op jit(solution)/shard_map/all_to_all | solution.py:34
  43.1 0.7 %copy-done.3 = f32[128]{0:T(128)S(1)} copy-done((f32[128]{0:T(128)S(1)}, f32[128]{0:T(128)}, u32[]{:S(2)}) %copy-start.3) | copy-done | bytes 536
  43.9 0.6 %copy-done.4 = f32[128]{0:T(128)S(1)} copy-done((f32[128]{0:T(128)S(1)}, f32[128]{0:T(128)}, u32[]{:S(2)}) %copy-start.4) | copy-done | bytes 536
  44.6 6.2 %all-to-all-done.1 = f32[4,1,32768]{2,1,0:T(1,128)S(1)} async-done(((f32[4,1,32768]{2,1,0:T(1,128)}), f32[4,1,32768]{2,1,0:T(1,128)S(1)}, u32[]{:S(2)}, u32[]{:S(2)}) %all-to-all-start.1) | async-done | bytes 524320 | tf_op jit(solution)/shard_map/all_to_all | solution.py:34
  50.8 2.1 %reduce.1 = f32[4,32768]{1,0:T(4,128)S(1)} reduce(f32[4,1,32768]{2,1,0:T(1,128)S(1)} %all-to-all-done.1, f32[]{:T(128)} %broadcast.76), dimensions={1}, to_apply=%all_to_all.17.reduce_sub_computation | reduce | bytes 1048580 | tf_op jit(solution)/shard_map/all_to_all | solution.py:34
  52.9 0.5 reshape.48
  53.4 0.7 %copy.34 = f32[16,32,4,64]{3,2,1,0:T(4,128)S(1)} copy(f32[16,32,4,64]{3,0,1,2:T(8,128)S(1)} %bitcast.41) | data formatting | bytes 1048576 | tf_op jit(solution)/shard_map/all_to_all | solution.py:34
  54.1 0.6 %all_to_all.20 = f32[16,32,256]{2,1,0:T(8,128)S(1)} reshape(f32[16,32,4,64]{3,2,1,0:T(4,128)S(1)} %copy.34) | data formatting | bytes 1048576 | tf_op jit(solution)/shard_map/all_to_all | solution.py:34
  54.8 2.4 %convolution_multiply_fusion = f32[16,32,256]{2,1,0:T(8,128)} fusion(f32[16,32,256]{2,1,0:T(8,128)S(1)} %all_to_all.20, f32[256]{0:T(256)S(1)} %copy-done.2, f32[16,32]{1,0:T(8,128)S(1)} %broadcast_add_fusion), kind=kOutput, calls=%fused_computation.1 | convolution fusion | flops 404488192 | bytes 1051648 | tf_op jit(solution)/shard_map/dot_general | solution.py:14
  (23 shorter events, 1.7 us)
Async XLA Ops:
  0.0 1.0 %copy-start = (f32[128,16,64]{0,2,1:T(8,128)S(1)}, f32[128,16,64]{0,2,1:T(8,128)}, u32[]{:S(2)}) copy-start(f32[128,16,64]{0,2,1:T(8,128)} %param.4) | copy-start | bytes 1572868
  9.5 0.9 %copy-start.1 = (f32[1,16,16,64]{3,2,1,0:T(8,128)S(1)}, f32[1,16,16,64]{3,2,1,0:T(8,128)}, u32[]{:S(2)}) copy-start(f32[1,16,16,64]{3,2,1,0:T(8,128)} %copy.26) | copy-start | bytes 196612
  39.4 11.4 %all-to-all-start.1 = ((f32[4,1,32768]{2,1,0:T(1,128)}), f32[4,1,32768]{2,1,0:T(1,128)S(1)}, u32[]{:S(2)}, u32[]{:S(2)}) async-start(f32[4,1,32768]{2,1,0:T(1,128)} %reshape.47), calls=%async_computation.1 | async-start | bytes 1048576 | tf_op jit(solution)/shard_map/all_to_all | solution.py:34
  43.1 0.7 %copy-start.3 = (f32[128]{0:T(128)S(1)}, f32[128]{0:T(128)}, u32[]{:S(2)}) copy-start(f32[128]{0:T(128)} %param.6) | copy-start | bytes 1540
  43.8 0.7 %copy-start.4 = (f32[128]{0:T(128)S(1)}, f32[128]{0:T(128)}, u32[]{:S(2)}) copy-start(f32[128]{0:T(128)} %param.5) | copy-start | bytes 1540
  54.1 0.7 %copy-start.2 = (f32[256]{0:T(256)S(1)}, f32[256]{0:T(256)}, u32[]{:S(2)}) copy-start(f32[256]{0:T(256)} %param.7) | copy-start | bytes 3076
